TPU v7x, 32 devices: a whole 2x2x4 slice. The times are simulated.
32 devices in a mesh: rep: 4 (over x, y), dp: 8 (over z, core).
Axes of the slice: x: 2, y: 2, z: 4, core: 2. Of those that a mesh axis runs over, the one named last changes fastest.
Arguments:
- x: bfloat16 [32, 4096, 896], P(('rep', 'dp')), parts along dimension 0
- dy: bfloat16 [32, 4096, 896], P(('rep', 'dp')), parts along dimension 0
- w_gate: bfloat16 [2, 896, 2304], P(None, 'dp')
- w_up: bfloat16 [2, 896, 2304], P(None, 'dp')
- w_down: bfloat16 [2, 2304, 896], P(None, 'dp')
Outputs:
- output 1: bfloat16 [32, 4096, 896], P(('rep', 'dp')), parts along dimension 0
- output 2: bfloat16 [8, 896, 2304], P('rep', 'dp'), parts along dimension 0
- output 3: bfloat16 [8, 896, 2304], P('rep', 'dp'), parts along dimension 0
- output 4: bfloat16 [8, 2304, 896], P('rep', 'dp'), parts along dimension 0
There are 4 independent parts. A program takes and returns all parts, laid end to end along the dimension named above; an argument that names none is the same for every part.
All inputs are finite; a program needn't handle non-finite values.
Results may differ from a plain program's by a relative error of at most 0.018.
Values are sent between devices in bfloat16 or wider.
A program may use at most 2 GiB of HBM per device.

v0:
```python
import jax
import jax.numpy as jnp
from jax import lax

NAMES = ("w_gate", "w_up", "w_down")


def matmul(a, w):
    return jnp.dot(a, w, preferred_element_type=jnp.float32).astype(jnp.bfloat16)


def normed(h):
    wide = h.astype(jnp.float32)
    scale = lax.rsqrt(jnp.mean(wide**2, -1, keepdims=True) + 1e-6)
    return (wide * scale).astype(jnp.bfloat16)


def layer(h, w):
    a = normed(h)
    gate = jnp.dot(a, w["w_gate"], preferred_element_type=jnp.float32)
    up = jnp.dot(a, w["w_up"], preferred_element_type=jnp.float32)
    return h + matmul((jax.nn.silu(gate) * up).astype(jnp.bfloat16), w["w_down"])


def stack(weights, h):
    for number in range(weights["w_gate"].shape[0]):
        h = layer(h, {name: w[number] for name, w in weights.items()})
    return h


def solution(mesh):
    groups = mesh.shape["rep"]

    def step(x, dy, *weights):
        shape = x.shape
        x, dy = (t.reshape(groups, -1, *t.shape[1:]) for t in (x, dy))

        def of_a_group(x, dy):
            _, back = jax.vjp(stack, dict(zip(NAMES, weights, strict=True)), x)
            by_weights, by_x = back(dy)
            return (by_x, *(by_weights[name] for name in NAMES))

        by_x, *by_weights = jax.vmap(of_a_group)(x, dy)
        return (by_x.reshape(shape), *(t.reshape(-1, *t.shape[2:]) for t in by_weights))

    return step
```

profile of v0, /device:TPU:0, one launch (start us, length us, event | category | flops | bytes accessed | tf_op | source)
XLA Modules:
  0.0 1289.3 jit_solution(3313407802600065524)
XLA Ops:
  58.3 26.8 %fusion.214 = f32[4096,2304]{1,0:T(8,128)} fusion(bf16[1,896,2304]{2,1,0:T(8,128)(2,1)} %all-gather.30.cloned.1.call-done, bf16[1,4096,896]{2,1,0:T(8,128)(2,1)} %param.13, f32[4096]{0:T(1024)S(1)} %get-tuple-element.267), kind=kOutput, calls=%fused_computation.254 | convolution fusion | flops 16922443776 | bytes 49233920 | tf_op jit(solution)/vmap(jvp())/dot_general | solution.py:20
  85.1 20.0 %all-gather.32.cloned.1.call-done = bf16[1,896,2304]{2,1,0:T(8,128)(2,1)} async-done(((bf16[1,112,2304]{2,1,0:T(8,128)(2,1)}), bf16[1,896,2304]{2,1,0:T(8,128)(2,1)}) %all-gather.32.cloned.1.call-update) | async-done | bytes 4128784 | tf_op jit(solution)/vmap(jvp())/squeeze | solution.py:27
  105.1 38.9 %fusion.168 = (bf16[1,1,4096,2304]{3,2,1,0:T(8,128)(2,1)}, f32[4096,2304]{1,0:T(8,128)}) fusion(f32[4096,2304]{1,0:T(8,128)} %fusion.214, bf16[1,896,2304]{2,1,0:T(8,128)(2,1)} %all-gather.32.cloned.1.call-done, bf16[1,4096,896]{2,1,0:T(8,128)(2,1)} %param.13, f32[4096]{0:T(1024)S(1)} %get-tuple-element.267), kind=kOutput, calls=%fused_computation.195 | convolution fusion | flops 16979066880 | bytes 105857024 | tf_op jit(solution)/vmap(jvp())/dot_general | solution.py:21
  151.8 23.4 %fusion.184 = (f32[4096]{0:T(1024)S(1)}, bf16[1,1,4096,896]{2,3,1,0:T(8,128)(2,1)S(1)}) fusion(bf16[1,2304,896]{2,1,0:T(8,128)(2,1)} %all-gather.34.cloned.1.call-done, bf16[1,1,4096,2304]{3,2,1,0:T(8,128)(2,1)} %get-tuple-element.268, bf16[1,4096,896]{1,2,0:T(8,128)(2,1)} %copy.1), kind=kOutput, calls=%fused_computation.227 | convolution fusion | flops 16929779712 | bytes 37699584 | tf_op jit(solution)/vmap(jvp())/dot_general | solution.py:9
  183.4 14.9 %all-gather.36.cloned.1.call-done = bf16[1,896,2304]{2,1,0:T(8,128)(2,1)} async-done(((bf16[1,112,2304]{2,1,0:T(8,128)(2,1)}), bf16[1,896,2304]{2,1,0:T(8,128)(2,1)}) %all-gather.36.cloned.1.call-update) | async-done | bytes 4128784 | tf_op jit(solution)/vmap(jvp())/squeeze | solution.py:27
  198.3 26.9 %fusion.195 = f32[4096,2304]{1,0:T(8,128)} fusion(bf16[1,1,4096,896]{2,3,1,0:T(8,128)(2,1)} %fusion.185, bf16[1,896,2304]{2,1,0:T(8,128)(2,1)} %all-gather.36.cloned.1.call-done), kind=kOutput, calls=%fused_computation.238 | convolution fusion | flops 16911433728 | bytes 49217536 | tf_op jit(solution)/vmap(jvp())/dot_general | solution.py:20
  225.3 19.6 %all-gather.40.cloned.1.call-done = bf16[1,896,2304]{2,1,0:T(8,128)(2,1)} async-done(((bf16[1,112,2304]{2,1,0:T(8,128)(2,1)}), bf16[1,896,2304]{2,1,0:T(8,128)(2,1)}) %all-gather.40.cloned.1.call-update) | async-done | bytes 4128784 | tf_op jit(solution)/vmap(jvp())/squeeze | solution.py:27
  244.9 42.4 %fusion.162 = (bf16[1,1,4096,2304]{3,2,1,0:T(8,128)(2,1)}, f32[4096,2304]{1,0:T(8,128)}) fusion(f32[4096,2304]{1,0:T(8,128)} %fusion.195, bf16[1,896,2304]{2,1,0:T(8,128)(2,1)} %all-gather.40.cloned.1.call-done, bf16[1,1,4096,896]{2,3,1,0:T(8,128)(2,1)} %fusion.185), kind=kOutput, calls=%fused_computation.185 | convolution fusion | flops 16968056832 | bytes 105840640 | tf_op jit(solution)/vmap(jvp())/dot_general | solution.py:21
  287.3 23.3 %copy.4 = bf16[1,1,4096,2304]{2,3,1,0:T(8,128)(2,1)} copy(bf16[1,1,4096,2304]{3,2,1,0:T(8,128)(2,1)} %get-tuple-element.268) | data formatting | bytes 37748736
  310.6 22.7 %copy.2 = bf16[1,1,4096,2304]{2,3,1,0:T(8,128)(2,1)} copy(bf16[1,1,4096,2304]{3,2,1,0:T(8,128)(2,1)} %get-tuple-element.275) | data formatting | bytes 37748736
  333.4 108.3 %while.16 = (bf16[1,1,4096,2304]{2,3,1,0:T(8,128)(2,1)}, bf16[1,1,4096,896]{3,2,1,0:T(8,128)(2,1)}, f32[1,288,896]{2,1,0:T(8,128)S(1)}, f32[1,288,896]{2,1,0:T(8...) while((bf16[1,1,4096,2304]{2,3,1,0:T(8,128)(2,1)}, ...), condition=%wide.windowed_dot_general_cond_rs.4.clone, body=%wide.windowed_dot_general_body_rs.4.clone.sunk | while | flops 8476139520 | bytes 89588320 | solution.py:9
  441.7 51.8 %convert_multiply_fusion.3 = (bf16[1,1,4096,2304]{3,2,1,0:T(8,128)(2,1)}, bf16[1,1,4096,2304]{3,2,1,0:T(8,128)(2,1)}) fusion(f32[4096,2304]{1,0:T(8,128)} %fusion.195, f32[4096,2304]{1,0:T(8,128)} %get-tuple-element.276, bf16[1,2304,896]{2,1,0:T(8,128)(2,1)} %all-gather.38.cloned.1.call-done, bf16[1,4096,896]{2,1,0:T(8,128)(2,1)} %param.12), kind=kOutput, calls=%fused_computation.173 | convolution fusion | flops 17062428672 | bytes 124715008 | tf_op jit(solution)/vmap(transpose(jvp()))/dot_general | solution.py:9
  493.5 22.8 %fusion.160 = bf16[4096,896]{0,1:T(8,128)(2,1)} fusion(bf16[1,1,4096,2304]{3,2,1,0:T(8,128)(2,1)} %get-tuple-element.551, bf16[1,896,2304]{2,1,0:T(8,128)(2,1)} %all-gather.36.cloned.1.call-done), kind=kOutput, calls=%fused_computation.182 | convolution fusion | flops 16911433728 | bytes 30343168 | tf_op jit(solution)/vmap(transpose(jvp()))/dot_general | solution.py:20
  516.3 28.1 %fusion.186 = (f32[4096]{0:T(1024)S(1)}, bf16[4096,896]{0,1:T(8,128)(2,1)}) fusion(bf16[1,1,4096,896]{2,3,1,0:T(8,128)(2,1)} %copy-done.12, bf16[4096,896]{0,1:T(8,128)(2,1)} %fusion.160, bf16[1,896,2304]{2,1,0:T(8,128)(2,1)} %all-gather.40.cloned.1.call-done, bf16[1,1,4096,2304]{3,2,1,0:T(8,128)(2,1)} %get-tuple-element.629), kind=kOutput, calls=%fused_computation.229 | convolution fusion | flops 16929779712 | bytes 45039616 | tf_op jit(solution)/vmap(transpose(jvp()))/dot_general | solution.py:21
  544.4 12.3 fusion.189
  567.7 109.9 %while.17 = (bf16[1,1,4096,2304]{2,3,1,0:T(8,128)(2,1)}, bf16[1,1,4096,896]{3,2,1,0:T(8,128)(2,1)}, f32[1,288,896]{2,1,0:T(8,128)S(1)}, f32[1,288,896]{2,1,0:T(8...) while((bf16[1,1,4096,2304]{2,3,1,0:T(8,128)(2,1)}, ...), condition=%wide.windowed_dot_general_cond_rs.5.clone, body=%wide.windowed_dot_general_body_rs.5.clone.sunk | while | flops 8476139520 | bytes 89588320 | solution.py:9
  609.4 12.5 collective-permute-done.22
  678.6 118.4 %while.14 = (bf16[1,1,4096,896]{2,3,1,0:T(8,128)(2,1)}, bf16[1,1,4096,2304]{3,2,1,0:T(8,128)(2,1)}, f32[1,112,2304]{2,1,0:T(8,128)S(1)}, f32[1,112,2304]{2,1,0:T...) while((bf16[1,1,4096,896]{2,3,1,0:T(8,128)(2,1)}, ...), condition=%wide.windowed_dot_general_cond_rs.2.clone, body=%wide.windowed_dot_general_body_rs.2.clone.sunk | while | flops 8464605184 | bytes 89588320 | solution.py:21
  695.5 20.1 %collective-permute-done.8 = f32[1,112,2304]{2,1,0:T(8,128)} collective-permute-done((f32[1,112,2304]{2,1,0:T(8,128)S(1)}, f32[1,112,2304]{2,1,0:T(8,128)}, u32[]{:S(2)}, u32[]{:S(2)}) %collective-permute-start.8) | collective-permute-done | bytes 1032224 | tf_op jit(solution)/vmap(transpose(jvp()))/dot_general | solution.py:21
  783.9 12.0 collective-permute-done.10
  797.5 52.3 %convert_multiply_fusion.1 = (bf16[1,1,4096,2304]{3,2,1,0:T(8,128)(2,1)}, bf16[1,1,4096,2304]{3,2,1,0:T(8,128)(2,1)}) fusion(f32[4096,2304]{1,0:T(8,128)} %fusion.214, f32[4096,2304]{1,0:T(8,128)} %get-tuple-element.269, bf16[1,2304,896]{2,1,0:T(8,128)(2,1)} %all-gather.34.cloned.1.call-done, bf16[1,1,4096,896]{2,3,1,0:T(8,128)(2,1)} %fusion.189), kind=kOutput, calls=%fused_computation.171 | convolution fusion | flops 17062428672 | bytes 124715008 | tf_op jit(solution)/vmap(transpose(jvp()))/dot_general | solution.py:9
  849.8 22.7 %fusion.156 = bf16[4096,896]{0,1:T(8,128)(2,1)} fusion(bf16[1,1,4096,2304]{3,2,1,0:T(8,128)(2,1)} %get-tuple-element.512, bf16[1,896,2304]{2,1,0:T(8,128)(2,1)} %all-gather.30.cloned.1.call-done), kind=kOutput, calls=%fused_computation.178 | convolution fusion | flops 16911433728 | bytes 30343168 | tf_op jit(solution)/vmap(transpose(jvp()))/dot_general | solution.py:20
  872.6 30.4 %fusion.183 = (bf16[1,1,4096,896]{2,3,1,0:T(8,128)(2,1)}, f32[4096]{0:T(1024)}, bf16[4096,896]{0,1:T(8,128)(2,1)}) fusion(bf16[1,4096,896]{1,2,0:T(8,128)(2,1)} %copy.1, f32[4096]{0:T(1024)S(1)} %bitcast.576, bf16[4096,896]{0,1:T(8,128)(2,1)} %fusion.156, bf16[1,896,2304]{2,1,0:T(8,128)(2,1)} %all-gather.32.cloned.1.call-done, ...), kind=kOutput, calls=%fused_computation.226 | convolution fusion | flops 16937119744 | bytes 52396032 | tf_op jit(solution)/vmap(transpose(jvp()))/dot_general | solution.py:21
  902.9 108.6 %while.15 = (bf16[1,1,4096,896]{2,3,1,0:T(8,128)(2,1)}, bf16[1,1,4096,2304]{3,2,1,0:T(8,128)(2,1)}, f32[1,112,2304]{2,1,0:T(8,128)S(1)}, f32[1,112,2304]{2,1,0:T...) while((bf16[1,1,4096,896]{2,3,1,0:T(8,128)(2,1)}, ...), condition=%wide.windowed_dot_general_cond_rs.3.clone, body=%wide.windowed_dot_general_body_rs.3.clone.sunk | while | flops 8464605184 | bytes 89588320 | solution.py:21
  945.0 12.8 collective-permute-done.14
  999.0 12.3 collective-permute-done.14
  1013.5 110.7 %while.12 = (bf16[1,1,4096,896]{2,3,1,0:T(8,128)(2,1)}, bf16[1,1,4096,2304]{3,2,1,0:T(8,128)(2,1)}, f32[1,112,2304]{2,1,0:T(8,128)S(1)}, f32[1,112,2304]{2,1,0:T...) while((bf16[1,1,4096,896]{2,3,1,0:T(8,128)(2,1)}, ...), condition=%wide.windowed_dot_general_cond_rs.clone, body=%wide.windowed_dot_general_body_rs.clone.sunk | while | flops 8464605184 | bytes 89588320 | solution.py:20
  1055.6 11.7 collective-permute-done.2
  1124.2 105.7 %while.13 = (bf16[1,1,4096,896]{2,3,1,0:T(8,128)(2,1)}, bf16[1,1,4096,2304]{3,2,1,0:T(8,128)(2,1)}, f32[1,112,2304]{2,1,0:T(8,128)S(1)}, f32[1,112,2304]{2,1,0:T...) while((bf16[1,1,4096,896]{2,3,1,0:T(8,128)(2,1)}, ...), condition=%wide.windowed_dot_general_cond_rs.1.clone, body=%wide.windowed_dot_general_body_rs.1.clone.sunk | while | flops 8464605184 | bytes 89588320 | solution.py:20
  1164.9 11.9 collective-permute-done.6
  1217.7 12.0 collective-permute-done.6
  1230.9 12.5 fusion.188
  (296 shorter events, 652.7 us)
Async XLA Ops:
  7.2 51.2 %all-gather.30.cloned.1.call-start = ((), (), s32[]{:S(2)}) async-start(), calls=%async_computation | async-start | bytes 4644864 | tf_op jit(solution)/vmap(jvp())/squeeze | solution.py:27
  9.5 95.6 %all-gather.32.cloned.1.call-start = ((), (), s32[]{:S(2)}) async-start(), calls=%async_computation.1 | async-start | bytes 4644864 | tf_op jit(solution)/vmap(jvp())/squeeze | solution.py:27
  11.8 139.9 %all-gather.34.cloned.1.call-start = ((), (), s32[]{:S(2)}) async-start(), calls=%async_computation.2 | async-start | bytes 4644864 | tf_op jit(solution)/vmap(jvp())/squeeze | solution.py:27
  14.2 184.2 %all-gather.36.cloned.1.call-start = ((), (), s32[]{:S(2)}) async-start(), calls=%async_computation.3 | async-start | bytes 4644864 | tf_op jit(solution)/vmap(jvp())/squeeze | solution.py:27
  14.7 230.2 %all-gather.40.cloned.1.call-start = ((), (), s32[]{:S(2)}) async-start(), calls=%async_computation.5 | async-start | bytes 4644864 | tf_op jit(solution)/vmap(jvp())/squeeze | solution.py:27
  15.3 426.4 %all-gather.38.cloned.1.call-start = ((), (), s32[]{:S(2)}) async-start(), calls=%async_computation.4 | async-start | bytes 4644864 | tf_op jit(solution)/vmap(jvp())/squeeze | solution.py:27
  333.6 26.7 %collective-permute-start.16 = (f32[1,288,896]{2,1,0:T(8,128)S(1)}, f32[1,288,896]{2,1,0:T(8,128)}, u32[]{:S(2)}, u32[]{:S(2)}) collective-permute-start(f32[1,288,896]{2,1,0:T(8,128)S(1)} %broadcast_select_fusion.32), channel_id=39, source_target_pairs={{0,1},{1,2},{2,3},{3,4},{4,5},{5,6},{6,7},{7,0},{8,9},{9,10},{10,1... | collective-permute-start | bytes 3096584 | tf_op jit(solution)/vmap(transpose(jvp()))/dot_general | solution.py:9
  334.0 26.4 %collective-permute-start.17 = (f32[1,288,896]{2,1,0:T(8,128)S(1)}, f32[1,288,896]{2,1,0:T(8,128)S(1)}, u32[]{:S(2)}, u32[]{:S(2)}) collective-permute-start(f32[1,288,896]{2,1,0:T(8,128)S(1)} %broadcast_select_fusion.33), channel_id=38, source_target_pairs={{0,7},{1,0},{2,1},{3,2},{4,3},{5,4},{6,5},{7,6},{8,15},{9,8},{10,9... | collective-permute-start | bytes 3096584 | tf_op jit(solution)/vmap(transpose(jvp()))/dot_general | solution.py:9
  361.8 25.5 %collective-permute-start.18 = (f32[1,288,896]{2,1,0:T(8,128)S(1)}, f32[1,288,896]{2,1,0:T(8,128)S(1)}, u32[]{:S(2)}, u32[]{:S(2)}) collective-permute-start(f32[1,288,896]{2,1,0:T(8,128)S(1)} %get-tuple-element.498), channel_id=41, source_target_pairs={{0,1},{1,2},{2,3},{3,4},{4,5},{5,6},{6,7},{7,0},{8,9},{9,10},{10,1... | collective-permute-start | bytes 3096584 | tf_op jit(solution)/vmap(transpose(jvp()))/dot_general | solution.py:9
  361.8 25.4 %collective-permute-start.19 = (f32[1,288,896]{2,1,0:T(8,128)S(1)}, f32[1,288,896]{2,1,0:T(8,128)S(1)}, u32[]{:S(2)}, u32[]{:S(2)}) collective-permute-start(f32[1,288,896]{2,1,0:T(8,128)S(1)} %get-tuple-element.499), channel_id=40, source_target_pairs={{0,7},{1,0},{2,1},{3,2},{4,3},{5,4},{6,5},{7,6},{8,15},{9,8},{10,9... | collective-permute-start | bytes 3096584 | tf_op jit(solution)/vmap(transpose(jvp()))/dot_general | solution.py:9
  441.7 812.5 %collective-permute-start.28 = (f32[1,288,896]{2,1,0:T(8,128)}, f32[1,288,896]{2,1,0:T(8,128)}, u32[]{:S(2)}, u32[]{:S(2)}) collective-permute-start(f32[1,288,896]{2,1,0:T(8,128)} %get-tuple-element.45), channel_id=42, source_target_pairs={{0,1},{1,2},{2,3},{3,4},{4,5},{5,6},{6,7},{7,0},{8,9},{9,10},{10,1... | collective-permute-start | bytes 3096584 | tf_op jit(solution)/vmap(transpose(jvp()))/dot_general | solution.py:9
  568.3 25.3 %collective-permute-start.20 = (f32[1,288,896]{2,1,0:T(8,128)S(1)}, f32[1,288,896]{2,1,0:T(8,128)}, u32[]{:S(2)}, u32[]{:S(2)}) collective-permute-start(f32[1,288,896]{2,1,0:T(8,128)S(1)} %broadcast_select_fusion.34), channel_id=45, source_target_pairs={{0,1},{1,2},{2,3},{3,4},{4,5},{5,6},{6,7},{7,0},{8,9},{9,10},{10,1... | collective-permute-start | bytes 3096584 | tf_op jit(solution)/vmap(transpose(jvp()))/dot_general | solution.py:9
  595.1 26.9 %collective-permute-start.22 = (f32[1,288,896]{2,1,0:T(8,128)S(1)}, f32[1,288,896]{2,1,0:T(8,128)S(1)}, u32[]{:S(2)}, u32[]{:S(2)}) collective-permute-start(f32[1,288,896]{2,1,0:T(8,128)S(1)} %get-tuple-element.507), channel_id=47, source_target_pairs={{0,1},{1,2},{2,3},{3,4},{4,5},{5,6},{6,7},{7,0},{8,9},{9,10},{10,1... | collective-permute-start | bytes 3096584 | tf_op jit(solution)/vmap(transpose(jvp()))/dot_general | solution.py:9
  596.2 25.8 %collective-permute-start.23 = (f32[1,288,896]{2,1,0:T(8,128)S(1)}, f32[1,288,896]{2,1,0:T(8,128)S(1)}, u32[]{:S(2)}, u32[]{:S(2)}) collective-permute-start(f32[1,288,896]{2,1,0:T(8,128)S(1)} %get-tuple-element.508), channel_id=46, source_target_pairs={{0,7},{1,0},{2,1},{3,2},{4,3},{5,4},{6,5},{7,6},{8,15},{9,8},{10,9... | collective-permute-start | bytes 3096584 | tf_op jit(solution)/vmap(transpose(jvp()))/dot_general | solution.py:9
  624.4 26.2 %collective-permute-start.20 = (f32[1,288,896]{2,1,0:T(8,128)S(1)}, f32[1,288,896]{2,1,0:T(8,128)}, u32[]{:S(2)}, u32[]{:S(2)}) collective-permute-start(f32[1,288,896]{2,1,0:T(8,128)S(1)} %broadcast_select_fusion.34), channel_id=45, source_target_pairs={{0,1},{1,2},{2,3},{3,4},{4,5},{5,6},{6,7},{7,0},{8,9},{9,10},{10,1... | collective-permute-start | bytes 3096584 | tf_op jit(solution)/vmap(transpose(jvp()))/dot_general | solution.py:9
  677.6 578.4 %collective-permute-start.29 = (f32[1,288,896]{2,1,0:T(8,128)}, f32[1,288,896]{2,1,0:T(8,128)}, u32[]{:S(2)}, u32[]{:S(2)}) collective-permute-start(f32[1,288,896]{2,1,0:T(8,128)} %get-tuple-element.47), channel_id=48, source_target_pairs={{0,1},{1,2},{2,3},{3,4},{4,5},{5,6},{6,7},{7,0},{8,9},{9,10},{10,1... | collective-permute-start | bytes 3096584 | tf_op jit(solution)/vmap(transpose(jvp()))/dot_general | solution.py:9
  678.8 36.8 %collective-permute-start.8 = (f32[1,112,2304]{2,1,0:T(8,128)S(1)}, f32[1,112,2304]{2,1,0:T(8,128)}, u32[]{:S(2)}, u32[]{:S(2)}) collective-permute-start(f32[1,112,2304]{2,1,0:T(8,128)S(1)} %broadcast_select_fusion.28), channel_id=27, source_target_pairs={{0,1},{1,2},{2,3},{3,4},{4,5},{5,6},{6,7},{7,0},{8,9},{9,10},{10,1... | collective-permute-start | bytes 3096584 | tf_op jit(solution)/vmap(transpose(jvp()))/dot_general | solution.py:21
  680.1 35.4 %collective-permute-start.9 = (f32[1,112,2304]{2,1,0:T(8,128)}, f32[1,112,2304]{2,1,0:T(8,128)S(1)}, u32[]{:S(2)}, u32[]{:S(2)}) collective-permute-start(f32[1,112,2304]{2,1,0:T(8,128)} %broadcast_select_fusion.29), channel_id=26, source_target_pairs={{0,7},{1,0},{2,1},{3,2},{4,3},{5,4},{6,5},{7,6},{8,15},{9,8},{10,9... | collective-permute-start | bytes 3096584 | tf_op jit(solution)/vmap(transpose(jvp()))/dot_general | solution.py:21
  742.9 26.5 %collective-permute-start.8 = (f32[1,112,2304]{2,1,0:T(8,128)S(1)}, f32[1,112,2304]{2,1,0:T(8,128)}, u32[]{:S(2)}, u32[]{:S(2)}) collective-permute-start(f32[1,112,2304]{2,1,0:T(8,128)S(1)} %broadcast_select_fusion.28), channel_id=27, source_target_pairs={{0,1},{1,2},{2,3},{3,4},{4,5},{5,6},{6,7},{7,0},{8,9},{9,10},{10,1... | collective-permute-start | bytes 3096584 | tf_op jit(solution)/vmap(transpose(jvp()))/dot_general | solution.py:21
  797.0 461.7 %collective-permute-start.26 = (f32[1,112,2304]{2,1,0:T(8,128)}, f32[1,112,2304]{2,1,0:T(8,128)}, u32[]{:S(2)}, u32[]{:S(2)}) collective-permute-start(f32[1,112,2304]{2,1,0:T(8,128)} %get-tuple-element.41), channel_id=30, source_target_pairs={{0,1},{1,2},{2,3},{3,4},{4,5},{5,6},{6,7},{7,0},{8,9},{9,10},{10,1... | collective-permute-start | bytes 3096584 | tf_op jit(solution)/vmap(transpose(jvp()))/dot_general | solution.py:21
  904.0 26.5 %collective-permute-start.12 = (f32[1,112,2304]{2,1,0:T(8,128)}, f32[1,112,2304]{2,1,0:T(8,128)}, u32[]{:S(2)}, u32[]{:S(2)}) collective-permute-start(f32[1,112,2304]{2,1,0:T(8,128)} %broadcast_select_fusion.30), channel_id=33, source_target_pairs={{0,1},{1,2},{2,3},{3,4},{4,5},{5,6},{6,7},{7,0},{8,9},{9,10},{10,1... | collective-permute-start | bytes 3096584 | tf_op jit(solution)/vmap(transpose(jvp()))/dot_general | solution.py:21
  904.2 26.4 %collective-permute-start.13 = (f32[1,112,2304]{2,1,0:T(8,128)S(1)}, f32[1,112,2304]{2,1,0:T(8,128)S(1)}, u32[]{:S(2)}, u32[]{:S(2)}) collective-permute-start(f32[1,112,2304]{2,1,0:T(8,128)S(1)} %broadcast_select_fusion.31), channel_id=32, source_target_pairs={{0,7},{1,0},{2,1},{3,2},{4,3},{5,4},{6,5},{7,6},{8,15},{9,8},{10,9... | collective-permute-start | bytes 3096584 | tf_op jit(solution)/vmap(transpose(jvp()))/dot_general | solution.py:21
  932.0 25.9 %collective-permute-start.14 = (f32[1,112,2304]{2,1,0:T(8,128)S(1)}, f32[1,112,2304]{2,1,0:T(8,128)S(1)}, u32[]{:S(2)}, u32[]{:S(2)}) collective-permute-start(f32[1,112,2304]{2,1,0:T(8,128)S(1)} %get-tuple-element.489), channel_id=35, source_target_pairs={{0,1},{1,2},{2,3},{3,4},{4,5},{5,6},{6,7},{7,0},{8,9},{9,10},{10,1... | collective-permute-start | bytes 3096584 | tf_op jit(solution)/vmap(transpose(jvp()))/dot_general | solution.py:21
  932.0 25.8 %collective-permute-start.15 = (f32[1,112,2304]{2,1,0:T(8,128)S(1)}, f32[1,112,2304]{2,1,0:T(8,128)S(1)}, u32[]{:S(2)}, u32[]{:S(2)}) collective-permute-start(f32[1,112,2304]{2,1,0:T(8,128)S(1)} %get-tuple-element.490), channel_id=34, source_target_pairs={{0,7},{1,0},{2,1},{3,2},{4,3},{5,4},{6,5},{7,6},{8,15},{9,8},{10,9... | collective-permute-start | bytes 3096584 | tf_op jit(solution)/vmap(transpose(jvp()))/dot_general | solution.py:21
  959.1 25.4 %collective-permute-start.12 = (f32[1,112,2304]{2,1,0:T(8,128)}, f32[1,112,2304]{2,1,0:T(8,128)}, u32[]{:S(2)}, u32[]{:S(2)}) collective-permute-start(f32[1,112,2304]{2,1,0:T(8,128)} %broadcast_select_fusion.30), channel_id=33, source_target_pairs={{0,1},{1,2},{2,3},{3,4},{4,5},{5,6},{6,7},{7,0},{8,9},{9,10},{10,1... | collective-permute-start | bytes 3096584 | tf_op jit(solution)/vmap(transpose(jvp()))/dot_general | solution.py:21
  959.2 25.3 %collective-permute-start.13 = (f32[1,112,2304]{2,1,0:T(8,128)S(1)}, f32[1,112,2304]{2,1,0:T(8,128)S(1)}, u32[]{:S(2)}, u32[]{:S(2)}) collective-permute-start(f32[1,112,2304]{2,1,0:T(8,128)S(1)} %broadcast_select_fusion.31), channel_id=32, source_target_pairs={{0,7},{1,0},{2,1},{3,2},{4,3},{5,4},{6,5},{7,6},{8,15},{9,8},{10,9... | collective-permute-start | bytes 3096584 | tf_op jit(solution)/vmap(transpose(jvp()))/dot_general | solution.py:21
  985.9 25.4 %collective-permute-start.14 = (f32[1,112,2304]{2,1,0:T(8,128)S(1)}, f32[1,112,2304]{2,1,0:T(8,128)S(1)}, u32[]{:S(2)}, u32[]{:S(2)}) collective-permute-start(f32[1,112,2304]{2,1,0:T(8,128)S(1)} %get-tuple-element.489), channel_id=35, source_target_pairs={{0,1},{1,2},{2,3},{3,4},{4,5},{5,6},{6,7},{7,0},{8,9},{9,10},{10,1... | collective-permute-start | bytes 3096584 | tf_op jit(solution)/vmap(transpose(jvp()))/dot_general | solution.py:21
  986.0 25.3 %collective-permute-start.15 = (f32[1,112,2304]{2,1,0:T(8,128)S(1)}, f32[1,112,2304]{2,1,0:T(8,128)S(1)}, u32[]{:S(2)}, u32[]{:S(2)}) collective-permute-start(f32[1,112,2304]{2,1,0:T(8,128)S(1)} %get-tuple-element.490), channel_id=34, source_target_pairs={{0,7},{1,0},{2,1},{3,2},{4,3},{5,4},{6,5},{7,6},{8,15},{9,8},{10,9... | collective-permute-start | bytes 3096584 | tf_op jit(solution)/vmap(transpose(jvp()))/dot_general | solution.py:21
  1015.0 26.1 %collective-permute-start = (f32[1,112,2304]{2,1,0:T(8,128)}, f32[1,112,2304]{2,1,0:T(8,128)}, u32[]{:S(2)}, u32[]{:S(2)}) collective-permute-start(f32[1,112,2304]{2,1,0:T(8,128)} %broadcast_select_fusion.24), channel_id=15, source_target_pairs={{0,1},{1,2},{2,3},{3,4},{4,5},{5,6},{6,7},{7,0},{8,9},{9,10},{10,1... | collective-permute-start | bytes 3096584 | tf_op jit(solution)/vmap(transpose(jvp()))/dot_general | solution.py:20
  1070.8 26.1 %collective-permute-start = (f32[1,112,2304]{2,1,0:T(8,128)}, f32[1,112,2304]{2,1,0:T(8,128)}, u32[]{:S(2)}, u32[]{:S(2)}) collective-permute-start(f32[1,112,2304]{2,1,0:T(8,128)} %broadcast_select_fusion.24), channel_id=15, source_target_pairs={{0,1},{1,2},{2,3},{3,4},{4,5},{5,6},{6,7},{7,0},{8,9},{9,10},{10,1... | collective-permute-start | bytes 3096584 | tf_op jit(solution)/vmap(transpose(jvp()))/dot_general | solution.py:20
  1229.9 30.1 %collective-permute-start.27 = (f32[1,112,2304]{2,1,0:T(8,128)}, f32[1,112,2304]{2,1,0:T(8,128)}, u32[]{:S(2)}, u32[]{:S(2)}) collective-permute-start(f32[1,112,2304]{2,1,0:T(8,128)} %copy-done.16), channel_id=36, source_target_pairs={{0,1},{1,2},{2,3},{3,4},{4,5},{5,6},{6,7},{7,0},{8,9},{9,10},{10,1... | collective-permute-start | bytes 3096584 | tf_op jit(solution)/vmap(transpose(jvp()))/dot_general | solution.py:21
  1254.3 26.9 %collective-permute-start.25 = (f32[1,112,2304]{2,1,0:T(8,128)}, f32[1,112,2304]{2,1,0:T(8,128)S(1)}, u32[]{:S(2)}, u32[]{:S(2)}) collective-permute-start(f32[1,112,2304]{2,1,0:T(8,128)} %copy-done.14), channel_id=24, source_target_pairs={{0,1},{1,2},{2,3},{3,4},{4,5},{5,6},{6,7},{7,0},{8,9},{9,10},{10,1... | collective-permute-start | bytes 3096584 | tf_op jit(solution)/vmap(transpose(jvp()))/dot_general | solution.py:20
  (58 other events, 1890.5 us)
Sparse Core Ops, SparseCore 0:
  9.6 48.6 all-gather.29
  60.0 45.0 all-gather.31
  106.7 45.0 all-gather.33
  153.3 45.0 all-gather.35
  199.8 45.0 all-gather.39
  246.4 45.0 all-gather.37
where the time goes:
time: 1300 us; the launch traced here: 1290 us
  matrix products  604 us (46%)
  waiting for transfers between devices  348 us (27%)
  local copies, waits for them, and re-layouts  121 us (9%)
  other arithmetic  89.9 us (7%)
  starting transfers between devices  87.3 us (7%)
  loops' own time  24.9 us (2%)
  between operations  14.6 us (1%)
    dot_general x12, matrix products, layer(): up = jnp.dot(a, w['w_up'], preferred_element_type=jnp.float32)  215 us
    dot_general x11, matrix products, matmul(): jnp.dot(a, w, preferred_element_type=jnp.float32).astype(jnp.bfloat16)  213 us
    dot_general x12, matrix products, layer(): gate = jnp.dot(a, w['w_gate'], preferred_element_type=jnp.float32)  175 us
    unnamed x67, local copies, waits for them, and re-layouts  106 us
    dot_general x18, waiting for transfers between devices, layer(): gate = jnp.dot(a, w['w_gate'], preferred_element_type=jnp.float32)  104 us
    dot_general x18, waiting for transfers between devices, layer(): up = jnp.dot(a, w['w_up'], preferred_element_type=jnp.float32)  98 us
    dot_general x18, waiting for transfers between devices, matmul(): jnp.dot(a, w, preferred_element_type=jnp.float32).astype(jnp.bfloat16)  77.1 us
    squeeze x6, waiting for transfers between devices, stack(): h = layer(h, {name: w[number] for name, w in weights.items()})  67.3 us
  transfers between devices with their start and end apart: 60, of which 31 were waited for; matrix products, arithmetic and copies ran while one was open for 62% of the time, Pallas kernels for 0%

commit v1 on v0

v1 whole, which is shorter than its diff:
```python
import functools

import jax
import jax.numpy as jnp
from jax import lax
from jax.experimental import pallas as pl
from jax.experimental.pallas import tpu as pltpu
from jax.sharding import PartitionSpec as P

TOK, D, FF, L, DP = 4096, 896, 2304, 2, 8
CW = 256
NCH = FF // CW
KR = FF // DP // NCH
DR = D // DP
T = 1024
NT = TOK // T
SUB = 256
NP = L * NCH
EPS = 1e-6
MESH = pl.DeviceIdType.MESH
F32, BF16 = jnp.float32, jnp.bfloat16
VMEM_LIMIT = 60 * 1024 * 1024


def dot(a, b, ca, cb):
    return lax.dot_general(a, b, (((ca,), (cb,)), ((), ())), preferred_element_type=F32)


def sigmoid(g):
    return 0.5 * jnp.tanh(0.5 * g) + 0.5


def scale_of(h):
    return lax.rsqrt(jnp.mean(h * h, -1, keepdims=True) + EPS)


def forward_kernel(x_ref, wg_ref, wu_ref, wd_ref, g_ref, u_ref, h_ref, a_s, acc):
    c = pl.program_id(1)

    @pl.when(c == 0)
    def _():
        for i in range(T // SUB):
            rows = pl.ds(i * SUB, SUB)
            h = x_ref[rows, :].astype(F32)
            a_s[rows, :] = (h * scale_of(h)).astype(BF16)
        acc[...] = jnp.zeros_like(acc)

    wg = wg_ref[:, 0, c].reshape(D, CW)
    wu = wu_ref[:, 0, c].reshape(D, CW)
    wd = wd_ref[:, 0, c].reshape(CW, D)
    for i in range(T // SUB):
        rows = pl.ds(i * SUB, SUB)
        a = a_s[rows, :]
        g = dot(a, wg, 1, 0)
        u = dot(a, wu, 1, 0)
        g_ref[rows, :] = g
        u_ref[rows, :] = u
        p = (g * sigmoid(g) * u).astype(BF16)
        acc[rows, :] += dot(p, wd, 1, 0)

    @pl.when(c == NCH - 1)
    def _():
        h_ref[...] = x_ref[...] + acc[...].astype(BF16)


def forward(x, wg, wu, wd):
    whole = lambda *s: pl.BlockSpec(s, lambda t, c: (0, 0, 0, 0, 0))
    return pl.pallas_call(
        forward_kernel,
        grid=(NT, NCH),
        in_specs=[
            pl.BlockSpec((T, D), lambda t, c: (t, 0)),
            whole(DP, 1, NCH, DR, CW),
            whole(DP, 1, NCH, DR, CW),
            whole(DP, 1, NCH, KR, D),
        ],
        out_specs=[
            pl.BlockSpec((T, CW), lambda t, c: (t, c)),
            pl.BlockSpec((T, CW), lambda t, c: (t, c)),
            pl.BlockSpec((T, D), lambda t, c: (t, 0)),
        ],
        out_shape=[
            jax.ShapeDtypeStruct((TOK, FF), F32),
            jax.ShapeDtypeStruct((TOK, FF), F32),
            jax.ShapeDtypeStruct((TOK, D), BF16),
        ],
        scratch_shapes=[pltpu.VMEM((T, D), BF16), pltpu.VMEM((T, D), F32)],
        compiler_params=pltpu.CompilerParams(
            vmem_limit_bytes=VMEM_LIMIT, dimension_semantics=("arbitrary", "arbitrary")
        ),
        cost_estimate=pl.CostEstimate(flops=6 * TOK * D * FF, bytes_accessed=10**8, transcendentals=0),
        name="forward",
    )(x, wg, wu, wd)


def backward_kernel(
    x_ref, h_ref, dy_ref, g_ref, u_ref, wg_ref, wu_ref, wd_ref,
    dx_ref, ogu_ref, od_ref,
    a_s, dcur, da, p_s, dg_s, du_s, acc_g, acc_u, acc_d,
    st_gu, st_d, xs_gu, xs_d, xr_gu, xr_d, cs_gu, cs_d, cr_gu, cr_d, fo_gu, fo_d,
    in_sem, xs_sem, xr_sem, cs_sem, cr_sem, out_sem, xfree, cfree,
):
    p = pl.program_id(0)
    t = pl.program_id(1)
    rep = lax.axis_index("rep")
    me = lax.axis_index("dp")
    z, core = me // 2, me % 2
    partner = z * 2 + (1 - core)
    lo, hi = jnp.maximum(me - 2, 0), jnp.minimum(me + 2, DP - 1)

    @pl.when((p == 0) & (t == 0))
    def _():
        load = pltpu.make_async_copy(dy_ref, dcur, in_sem)
        load.start()
        barrier = pltpu.get_barrier_semaphore()
        pl.semaphore_signal(barrier, inc=1, device_id=(rep, partner), device_id_type=MESH)

        @pl.when(z > 0)
        def _():
            pl.semaphore_signal(barrier, inc=1, device_id=(rep, lo), device_id_type=MESH)

        @pl.when(z < 3)
        def _():
            pl.semaphore_signal(barrier, inc=1, device_id=(rep, hi), device_id_type=MESH)

        pl.semaphore_wait(barrier, jnp.where((z == 0) | (z == 3), 2, 3))
        load.wait()
        acc_g[...] = jnp.zeros_like(acc_g)
        acc_u[...] = jnp.zeros_like(acc_u)
        acc_d[...] = jnp.zeros_like(acc_d)

    def swap(b):
        return [
            pltpu.make_async_remote_copy(
                src_ref=s.at[b], dst_ref=r.at[b], send_sem=xs_sem.at[b, i], recv_sem=xr_sem.at[b, i],
                device_id=(rep, partner), device_id_type=MESH,
            )
            for i, (s, r) in enumerate(((xs_gu, xr_gu), (xs_d, xr_d)))
        ]

    def hop(b, way, s, to):
        return [
            pltpu.make_async_remote_copy(
                src_ref=o.at[b, way, s], dst_ref=r.at[b, way, s],
                send_sem=cs_sem.at[b, way, s, i], recv_sem=cr_sem.at[b, way, s, i],
                device_id=(rep, to), device_id_type=MESH,
            )
            for i, (o, r) in enumerate(((cs_gu, cr_gu), (cs_d, cr_d)))
        ]

    def out_copies(b, ph):
        lay, c = 1 - ph // NCH, ph % NCH
        return [
            pltpu.make_async_copy(fo_gu.at[b], ogu_ref.at[lay, c], out_sem.at[b, 0]),
            pltpu.make_async_copy(fo_d.at[b], od_ref.at[lay, c], out_sem.at[b, 1]),
        ]

    def give(r):
        b = r % 2

        @pl.when(r >= 2)
        def _():
            pl.semaphore_wait(xfree.at[b], 1)
            for cp in swap(b):
                cp.wait_send()

        for dz in range(4):
            j = dz * 2 + (1 - core)
            rows = pl.ds(pl.multiple_of(j * DR, 16), DR)
            xs_gu[b, dz, 0] = acc_g[rows, :].astype(BF16)
            xs_gu[b, dz, 1] = acc_u[rows, :].astype(BF16)
            xs_d[b, dz] = acc_d[pl.ds(pl.multiple_of(j * KR, 16), KR), :].astype(BF16)
        for cp in swap(b):
            cp.start()
        for dz in range(4):
            j = dz * 2 + core
            rows = pl.ds(pl.multiple_of(j * DR, 16), DR)
            st_gu[b, dz, 0] = acc_g[rows, :]
            st_gu[b, dz, 1] = acc_u[rows, :]
            st_d[b, dz] = acc_d[pl.ds(pl.multiple_of(j * KR, 16), KR), :]
        acc_g[...] = jnp.zeros_like(acc_g)
        acc_u[...] = jnp.zeros_like(acc_u)
        acc_d[...] = jnp.zeros_like(acc_d)

    def take(r):
        b = r % 2
        for cp in swap(b):
            cp.wait_recv()
        st_gu[b] += xr_gu[b].astype(F32)
        st_d[b] += xr_d[b].astype(F32)

        @pl.when(r < NP - 2)
        def _():
            pl.semaphore_signal(xfree.at[b], inc=1, device_id=(rep, partner), device_id_type=MESH)

    def send(r, s):
        b = r % 2
        for way in range(2):
            zz = z if way == 0 else 3 - z
            to = hi if way == 0 else lo

            @pl.when(zz <= s)
            def _(zz=zz, to=to, way=way):
                dest = 3 - s + zz
                dest = jnp.minimum(dest, 3)
                dest = dest if way == 0 else 3 - dest
                copies = hop(b, way, s, to)

                if s < 3:
                    @pl.when((r >= 2) & (zz == s))
                    def _():
                        pl.semaphore_wait(cfree.at[b, way], 1)

                    @pl.when(r >= 2)
                    def _():
                        for cp in copies:
                            cp.wait_send()

                @pl.when(zz == 0)
                def _():
                    cs_gu[b, way, s] = st_gu[b, dest].astype(BF16)
                    cs_d[b, way, s] = st_d[b, dest].astype(BF16)

                if s > 0:
                    @pl.when(zz > 0)
                    def _():
                        for cp in hop(b, way, s - 1, to):
                            cp.wait_recv()
                        cs_gu[b, way, s] = (st_gu[b, dest] + cr_gu[b, way, s - 1].astype(F32)).astype(BF16)
                        cs_d[b, way, s] = (st_d[b, dest] + cr_d[b, way, s - 1].astype(F32)).astype(BF16)

                for cp in copies:
                    cp.start()

    def finish(r):
        b = r % 2
        for way in range(2):
            zz = z if way == 0 else 3 - z
            to = hi if way == 0 else lo
            back = lo if way == 0 else hi

            @pl.when(zz > 0)
            def _(way=way, to=to, back=back):
                for cp in hop(b, way, 2, to):
                    cp.wait_recv()
                st_gu[b, z] += cr_gu[b, way, 2].astype(F32)
                st_d[b, z] += cr_d[b, way, 2].astype(F32)

                @pl.when(r < NP - 2)
                def _():
                    pl.semaphore_signal(cfree.at[b, way], inc=1, device_id=(rep, back), device_id_type=MESH)

        @pl.when(r >= 2)
        def _():
            for cp in out_copies(b, r - 2):
                cp.wait()

        fo_gu[b] = st_gu[b, z].astype(BF16)
        fo_d[b] = st_d[b, z].astype(BF16)
        for cp in out_copies(b, r):
            cp.start()

    @pl.when(p < NP)
    def compute():
        c = p % NCH
        tok = pl.multiple_of(t * T, T)

        def norm_into(src):
            for i in range(T // SUB):
                rows = pl.ds(i * SUB, SUB)
                h = src[rows, :].astype(F32)
                a_s[rows, :] = (h * scale_of(h)).astype(BF16)

        wg = wg_ref[...].reshape(D, CW)
        wu = wu_ref[...].reshape(D, CW)
        wd = wd_ref[...].reshape(CW, D)

        def elementwise(g, u, i):
            rows = pl.ds(i * SUB, SUB)
            dp = dot(dcur[pl.ds(tok + i * SUB, SUB), :], wd, 1, 1).astype(BF16).astype(F32)
            s = sigmoid(g)
            act = g * s
            p_s[rows, :] = (act * u).astype(BF16)
            du_s[rows, :] = (act * dp).astype(BF16)
            dg_s[rows, :] = (dp * u * (s + act * (1.0 - s))).astype(BF16)

        @pl.when(p < NCH)
        def _():
            norm_into(h_ref)
            for i in range(T // SUB):
                a = a_s[pl.ds(i * SUB, SUB), :]
                elementwise(dot(a, wg, 1, 0), dot(a, wu, 1, 0), i)

        @pl.when(p >= NCH)
        def _():
            norm_into(x_ref)
            for i in range(T // SUB):
                rows = pl.ds(i * SUB, SUB)
                elementwise(g_ref[rows, :], u_ref[rows, :], i)

        a = a_s[...]
        here = pl.ds(tok, T)
        acc_d[...] += dot(p_s[...], dcur[here, :], 0, 0)
        acc_g[...] += dot(a, dg_s[...], 0, 0)
        acc_u[...] += dot(a, du_s[...], 0, 0)

        @pl.when(c == 0)
        def _():
            da[here, :] = dot(dg_s[...], wg, 1, 1) + dot(du_s[...], wu, 1, 1)

        @pl.when(c > 0)
        def _():
            da[here, :] += dot(dg_s[...], wg, 1, 1) + dot(du_s[...], wu, 1, 1)

        def through_norm(src):
            for i in range(T // SUB):
                rows = pl.ds(i * SUB, SUB)
                glob = pl.ds(tok + i * SUB, SUB)
                h = src[rows, :].astype(F32)
                m = scale_of(h)
                d = da[glob, :].astype(BF16).astype(F32)
                k = jnp.sum(h * d, -1, keepdims=True) * (m * m * m) * (-1.0 / D)
                new = dcur[glob, :] + (d * m + h * k).astype(BF16)
                dcur[glob, :] = new
                dx_ref[rows, :] = new

        @pl.when(p == NCH - 1)
        def _():
            through_norm(h_ref)

        @pl.when(p == NP - 1)
        def _():
            through_norm(x_ref)

    one, two = (p >= 1) & (p - 1 < NP), (p >= 2) & (p - 2 < NP)

    @pl.when((t == 0) & two)
    def _():
        send(p - 2, 2)

    @pl.when((t == 0) & one)
    def _():
        take(p - 1)
        send(p - 1, 0)

    @pl.when((t == NT // 2) & two)
    def _():
        finish(p - 2)

    @pl.when((t == NT // 2) & one)
    def _():
        send(p - 1, 1)

    @pl.when((t == NT - 1) & (p < NP))
    def _():
        give(p)

    @pl.when((p == NP + 1) & (t == NT - 1))
    def _():
        for r in (NP - 2, NP - 1):
            b = r % 2
            for cp in swap(b):
                cp.wait_send()
            for way in range(2):
                zz = z if way == 0 else 3 - z
                for s in range(3):
                    @pl.when(zz <= s)
                    def _(way=way, s=s, b=b):
                        for cp in hop(b, way, s, hi if way == 0 else lo):
                            cp.wait_send()
            for cp in out_copies(b, r):
                cp.wait()


def backward(x, h, dy, g, u, wg, wu, wd):
    def phase(p):
        return jnp.minimum(p, NP - 1)

    def w_map(p, t):
        q = phase(p)
        return (0, 1 - q // NCH, q % NCH, 0, 0)

    late = lambda p, t: jnp.where(p >= NP, NT - 1, jnp.where(p >= NCH, t, 0))
    gu_spec = pl.BlockSpec((T, CW), lambda p, t: (late(p, t), jnp.where(p >= NCH, phase(p) % NCH, 0)))
    any_spec = pl.BlockSpec(memory_space=pl.ANY)
    vm = pltpu.VMEM
    return pl.pallas_call(
        backward_kernel,
        grid=(NP + 2, NT),
        in_specs=[
            pl.BlockSpec((T, D), lambda p, t: (late(p, t), 0)),
            pl.BlockSpec((T, D), lambda p, t: (jnp.where(p < NCH, t, NT - 1), 0)),
            any_spec,
            gu_spec,
            gu_spec,
            pl.BlockSpec((DP, None, None, DR, CW), w_map),
            pl.BlockSpec((DP, None, None, DR, CW), w_map),
            pl.BlockSpec((DP, None, None, KR, D), w_map),
        ],
        out_specs=[
            pl.BlockSpec((T, D), lambda p, t: (jnp.where(p >= NP, NT - 1, jnp.where(p == NP - 1, t, 0)), 0)),
            any_spec,
            any_spec,
        ],
        out_shape=[
            jax.ShapeDtypeStruct((TOK, D), BF16),
            jax.ShapeDtypeStruct((L, NCH, 2, DR, CW), BF16),
            jax.ShapeDtypeStruct((L, NCH, KR, D), BF16),
        ],
        scratch_shapes=[
            vm((T, D), BF16), vm((TOK, D), BF16), vm((TOK, D), F32),
            vm((T, CW), BF16), vm((T, CW), BF16), vm((T, CW), BF16),
            vm((D, CW), F32), vm((D, CW), F32), vm((CW, D), F32),
            vm((2, 4, 2, DR, CW), F32), vm((2, 4, KR, D), F32),
            vm((2, 4, 2, DR, CW), BF16), vm((2, 4, KR, D), BF16),
            vm((2, 4, 2, DR, CW), BF16), vm((2, 4, KR, D), BF16),
            vm((2, 2, 3, 2, DR, CW), BF16), vm((2, 2, 3, KR, D), BF16),
            vm((2, 2, 3, 2, DR, CW), BF16), vm((2, 2, 3, KR, D), BF16),
            vm((2, 2, DR, CW), BF16), vm((2, KR, D), BF16),
            pltpu.SemaphoreType.DMA,
            pltpu.SemaphoreType.DMA((2, 2)), pltpu.SemaphoreType.DMA((2, 2)),
            pltpu.SemaphoreType.DMA((2, 2, 3, 2)), pltpu.SemaphoreType.DMA((2, 2, 3, 2)),
            pltpu.SemaphoreType.DMA((2, 2)),
            pltpu.SemaphoreType.REGULAR((2,)), pltpu.SemaphoreType.REGULAR((2, 2)),
        ],
        compiler_params=pltpu.CompilerParams(
            vmem_limit_bytes=VMEM_LIMIT, collective_id=1, has_side_effects=True,
            dimension_semantics=("arbitrary", "arbitrary"),
        ),
        cost_estimate=pl.CostEstimate(flops=28 * TOK * D * FF, bytes_accessed=10**8, transcendentals=0),
        name="backward",
    )(x, h, dy, g, u, wg, wu, wd)


def solution(mesh):
    def body(x, dy, w_gate, w_up, w_down):
        x, dy = x[0], dy[0]
        split = lambda w: w.reshape(L, DR, DP, NCH, KR).transpose(0, 3, 1, 2, 4).reshape(L, NCH, DR, CW)
        gather = lambda w: lax.all_gather(w, "dp", axis=0, tiled=False)
        wg, wu = gather(split(w_gate)), gather(split(w_up))
        wd = gather(w_down.reshape(L, NCH, KR, D))
        g, u, h = forward(x, wg, wu, wd)
        dx, ogu, od = backward(x, h, dy, g, u, wg, wu, wd)
        join = lambda o: o.reshape(L, NCH, DR, DP, KR).transpose(0, 2, 3, 1, 4).reshape(L, DR, FF)
        return dx[None], join(ogu[:, :, 0]), join(ogu[:, :, 1]), od.reshape(L, NCH * KR, D)

    rows = P(None, "dp", None)
    seqs = P(("rep", "dp"), None, None)
    outs = P("rep", "dp", None)
    return jax.shard_map(
        body, mesh=mesh, in_specs=(seqs, seqs, rows, rows, rows), out_specs=(seqs, outs, outs, outs), check_vma=False
    )
```

time: 1300 us -> 786 us (0.60)
  matrix products: 604 us -> 0 us
  Pallas kernels: 0 us -> 509 us
  waiting for transfers between devices: 348 us -> 243 us
  local copies, waits for them, and re-layouts: 121 us -> 19.9 us
  other arithmetic: 89.9 us -> 0 us
  starting transfers between devices: 87.3 us -> 0.12 us
  loops' own time: 24.9 us -> 0 us
    dot_general x35 -> x0, matrix products: 604 us -> none  [the longest x12 215 us: layer(): up = jnp.dot(a, w['w_up'], preferred_element_type=jnp.float32)]
    pallas_call x0 -> x2, Pallas kernels: none -> 509 us  [the longest x1 415 us: backward(): pl.pallas_call(backward_kernel, grid=(NP + 2, NT), in_specs=[pl.BlockSpec...]
    dot_general x54 -> x0, waiting for transfers between devices: 279 us -> none  [the longest x18 104 us: layer(): gate = jnp.dot(a, w['w_gate'], preferred_element_type=jnp.float32)]
    all_gather x0 -> x3, waiting for transfers between devices: none -> 242 us  [body(): gather = lambda w: lax.all_gather(w, 'dp', axis=0, tiled=False)]
    unnamed x67 -> x10, local copies, waits for them, and re-layouts: 106 us -> 13 us
    dot_general x54 -> x0, starting transfers between devices: 87 us -> none  [the longest x18 29.2 us: layer(): up = jnp.dot(a, w['w_up'], preferred_element_type=jnp.float32)]
    squeeze x6 -> x0, waiting for transfers between devices: 67.3 us -> none  [stack(): h = layer(h, {name: w[number] for name, w in weights.items()})]
    dot_general x48 -> x0, other arithmetic: 45.8 us -> none
  transfers between devices with their start and end apart: 60 -> 3, of which waited for: 31 -> 3; matrix products, arithmetic and copies ran while one was open for 62% -> 1% of each run, Pallas kernels for 0% -> 0%
where the time goes in v1:
time: 786 us; the launch traced here: 785 us
  Pallas kernels  509 us (65%)
  waiting for transfers between devices  243 us (31%)
  local copies, waits for them, and re-layouts  19.9 us (3%)
  between operations  13.8 us (2%)
    pallas_call x1, Pallas kernels, backward(): pl.pallas_call(backward_kernel, grid=(NP + 2, NT), in_specs=[pl.BlockSpec...  415 us
    all_gather x3, waiting for transfers between devices, body(): gather = lambda w: lax.all_gather(w, 'dp', axis=0, tiled=False)  242 us
    pallas_call x1, Pallas kernels, forward(): pl.pallas_call(forward_kernel, grid=(NT, NCH), in_specs=[pl.BlockSpec((T,...  93.5 us
  transfers between devices with their start and end apart: 3, of which 3 were waited for; matrix products, arithmetic and copies ran while one was open for 1% of the time, Pallas kernels for 0%

profile of v1, /device:TPU:0, one launch (start us, length us, event | category | flops | bytes accessed | tf_op | source)
XLA Modules:
  0.0 785.3 jit_solution(9045034505948233912)
XLA Ops:
  7.2 0.0 copy-start
  7.2 0.0 all-gather.8.cloned.1.call-start
  7.2 0.7 all-gather.8.cloned.1.call-update
  7.9 0.0 all-gather.4.cloned.1.call-start
  8.0 1.7 copy.25
  9.7 0.3 copy.26
  10.0 1.4 copy.27
  11.4 0.0 all-gather.4.cloned.1.call-update
  11.4 0.0 all-gather.6.cloned.1.call-start
  11.4 0.0 copy-done
  11.4 0.8 copy.28
  12.2 0.3 copy.29
  12.5 1.4 copy.30
  13.9 0.0 all-gather.6.cloned.1.call-update
  13.9 78.9 %all-gather.8.cloned.1.call-done.wd_ref = bf16[8,2,9,32,896]{4,3,2,1,0:T(8,128)(2,1)} async-done(((bf16[1,2,9,32,896]{4,3,2,1,0:T(8,128)(2,1)}), bf16[8,2,9,32,896]{4,3,2,1,0:T(8,128)(2,1)}) %all-gather.8.cloned.1.call-update) | async-done | bytes 8257552 | tf_op jit(solution)/shard_map/all_gather | solution.py:439
  92.8 81.5 %all-gather.4.cloned.1.call-done.wg_ref = bf16[8,2,9,112,256]{4,3,2,1,0:T(8,128)(2,1)} async-done(((bf16[1,2,9,112,256]{4,3,2,1,0:T(8,128)(2,1)}), bf16[8,2,9,112,256]{4,3,2,1,0:T(8,128)(2,1)}) %all-gather.4.cloned.1.call-update) | async-done | bytes 8257552 | tf_op jit(solution)/shard_map/all_gather | solution.py:439
  174.3 81.5 %all-gather.6.cloned.1.call-done.wu_ref = bf16[8,2,9,112,256]{4,3,2,1,0:T(8,128)(2,1)} async-done(((bf16[1,2,9,112,256]{4,3,2,1,0:T(8,128)(2,1)}), bf16[8,2,9,112,256]{4,3,2,1,0:T(8,128)(2,1)}) %all-gather.6.cloned.1.call-update) | async-done | bytes 8257552 | tf_op jit(solution)/shard_map/all_gather | solution.py:439
  255.8 93.5 %forward.1 = (f32[4096,2304]{1,0:T(8,128)}, f32[4096,2304]{1,0:T(8,128)}, bf16[4096,896]{1,0:T(8,128)(2,1)}) custom-call(bf16[4096,896]{1,0:T(8,128)(2,1)} %bitcast.32, bf16[8,2,9,112,256]{4,3,2,1,0:T(8,128)(2,1)} %all-gather.4.cloned.1.call-done.wg_ref, bf16[8,2,9,112,256]{4,3,2,1,0:T(8,128)(2,1)} %all-gather.6.cloned.1.call-done.wu_ref, ...), custom_call_target="tpu_custom_call" | custom-call | flops 50734301184 | bytes 100000000 | tf_op jit(solution)/shard_map/forward/pallas_call | solution.py:68
  349.3 415.3 %backward.1 = (bf16[4096,896]{1,0:T(8,128)(2,1)}, bf16[2,9,2,112,256]{4,3,2,1,0:T(8,128)(2,1)}, bf16[2,9,32,896]{3,2,1,0:T(8,128)(2,1)}) custom-call(bf16[4096,896]{1,0:T(8,128)(2,1)} %bitcast.33, bf16[4096,896]{1,0:T(8,128)(2,1)} %get-tuple-element.10.h_ref, bf16[4096,896]{1,0:T(8,128)(2,1)} %bitcast.34, f32[4096,2304]{1,0:T(8,128)} %get-tuple-element.11.g_ref, ...), custom_call_target="tpu_custom_call" | custom-call | flops 236760072192 | bytes 100000000 | tf_op jit(solution)/shard_map/backward/pallas_call | solution.py:387
  764.7 1.7 fusion
  766.3 0.8 copy.33
  767.1 0.2 copy.34
  767.3 1.4 copy.36
  768.7 0.7 copy.31
  769.5 0.2 copy.32
  769.7 1.4 copy.35
  771.0 0.0 copy-start.1
  771.0 6.8 copy.39
  777.8 0.0 copy-done.1
  777.8 1.0 copy.40
Async XLA Ops:
  7.2 4.3 copy-start
  7.2 85.6 %all-gather.8.cloned.1.call-start = ((), (), s32[]{:S(2)}) async-start(), calls=%async_computation.2 | async-start | bytes 9289728 | tf_op jit(solution)/shard_map/all_gather | solution.py:439
  7.9 166.4 %all-gather.4.cloned.1.call-start = ((), (), s32[]{:S(2)}) async-start(), calls=%async_computation | async-start | bytes 9289728 | tf_op jit(solution)/shard_map/all_gather | solution.py:439
  11.4 244.4 %all-gather.6.cloned.1.call-start = ((), (), s32[]{:S(2)}) async-start(), calls=%async_computation.1 | async-start | bytes 9289728 | tf_op jit(solution)/shard_map/all_gather | solution.py:439
  771.0 6.8 copy-start.1
Sparse Core Ops, SparseCore 0:
  9.6 83.1 all-gather.7
  95.0 79.2 all-gather.3
  176.5 79.2 all-gather.5

commit v2 on v1

--- a/solution.py
+++ b/solution.py
@@ -15,11 +15,13 @@
 T = 1024
 NT = TOK // T
 SUB = 256
+FSUB = 256
+TB = 512
 NP = L * NCH
 EPS = 1e-6
 MESH = pl.DeviceIdType.MESH
 F32, BF16 = jnp.float32, jnp.bfloat16
-VMEM_LIMIT = 60 * 1024 * 1024
+VMEM_LIMIT = 67_043_328
 
 
 def dot(a, b, ca, cb):
@@ -34,69 +36,86 @@
     return lax.rsqrt(jnp.mean(h * h, -1, keepdims=True) + EPS)
 
 
-def forward_kernel(x_ref, wg_ref, wu_ref, wd_ref, g_ref, u_ref, h_ref, a_s, acc):
-    c = pl.program_id(1)
-
-    @pl.when(c == 0)
+def gate_up_kernel(keep_p, x_ref, wg_ref, wu_ref, *refs):
+    g_ref, u_ref, a_ref = refs[:3] if keep_p else refs[3:6]
+
+    @pl.when(pl.program_id(1) == 0)
     def _():
         for i in range(T // SUB):
             rows = pl.ds(i * SUB, SUB)
             h = x_ref[rows, :].astype(F32)
-            a_s[rows, :] = (h * scale_of(h)).astype(BF16)
-        acc[...] = jnp.zeros_like(acc)
-
-    wg = wg_ref[:, 0, c].reshape(D, CW)
-    wu = wu_ref[:, 0, c].reshape(D, CW)
-    wd = wd_ref[:, 0, c].reshape(CW, D)
-    for i in range(T // SUB):
-        rows = pl.ds(i * SUB, SUB)
-        a = a_s[rows, :]
+            a_ref[rows, :] = (h * scale_of(h)).astype(BF16)
+
+    wg = wg_ref[...].reshape(D, CW)
+    wu = wu_ref[...].reshape(D, CW)
+    for i in range(T // FSUB):
+        rows = pl.ds(i * FSUB, FSUB)
+        a = a_ref[rows, :]
         g = dot(a, wg, 1, 0)
         u = dot(a, wu, 1, 0)
         g_ref[rows, :] = g
         u_ref[rows, :] = u
-        p = (g * sigmoid(g) * u).astype(BF16)
-        acc[rows, :] += dot(p, wd, 1, 0)
-
-    @pl.when(c == NCH - 1)
-    def _():
-        h_ref[...] = x_ref[...] + acc[...].astype(BF16)
-
-
-def forward(x, wg, wu, wd):
-    whole = lambda *s: pl.BlockSpec(s, lambda t, c: (0, 0, 0, 0, 0))
+        if keep_p:
+            refs[3][rows, :] = (g * sigmoid(g) * u).astype(BF16)
+
+
+def gate_up(layer, x, wgu, *before):
+    keep_p = layer == 0
+    tile = pl.BlockSpec((None, T, CW), lambda t, c: (layer, t, c))
+    wide = jax.ShapeDtypeStruct((L, TOK, FF), F32)
+    p_spec, p_shape = [pl.BlockSpec((T, CW), lambda t, c: (t, c))], [jax.ShapeDtypeStruct((TOK, FF), BF16)]
     return pl.pallas_call(
-        forward_kernel,
+        functools.partial(gate_up_kernel, keep_p),
         grid=(NT, NCH),
         in_specs=[
             pl.BlockSpec((T, D), lambda t, c: (t, 0)),
-            whole(DP, 1, NCH, DR, CW),
-            whole(DP, 1, NCH, DR, CW),
-            whole(DP, 1, NCH, KR, D),
-        ],
-        out_specs=[
-            pl.BlockSpec((T, CW), lambda t, c: (t, c)),
-            pl.BlockSpec((T, CW), lambda t, c: (t, c)),
-            pl.BlockSpec((T, D), lambda t, c: (t, 0)),
-        ],
-        out_shape=[
-            jax.ShapeDtypeStruct((TOK, FF), F32),
-            jax.ShapeDtypeStruct((TOK, FF), F32),
-            jax.ShapeDtypeStruct((TOK, D), BF16),
-        ],
-        scratch_shapes=[pltpu.VMEM((T, D), BF16), pltpu.VMEM((T, D), F32)],
+            pl.BlockSpec((DP, None, DR, CW), lambda t, c: (0, c, 0, 0)),
+            pl.BlockSpec((DP, None, DR, CW), lambda t, c: (0, NCH + c, 0, 0)),
+        ] + [pl.BlockSpec(memory_space=pl.ANY)] * len(before),
+        out_specs=[tile, tile, pl.BlockSpec((None, T, D), lambda t, c: (layer, t, 0))] + p_spec * keep_p,
+        out_shape=[wide, wide, jax.ShapeDtypeStruct((L, TOK, D), BF16)] + p_shape * keep_p,
+        input_output_aliases={3 + i: i for i in range(len(before))},
         compiler_params=pltpu.CompilerParams(
             vmem_limit_bytes=VMEM_LIMIT, dimension_semantics=("arbitrary", "arbitrary")
         ),
-        cost_estimate=pl.CostEstimate(flops=6 * TOK * D * FF, bytes_accessed=10**8, transcendentals=0),
-        name="forward",
-    )(x, wg, wu, wd)
+        cost_estimate=pl.CostEstimate(flops=4 * TOK * D * FF, bytes_accessed=10**8, transcendentals=0),
+        name=f"gate_up_{layer}",
+    )(x, wgu, wgu, *before)
+
+
+def down_kernel(x_ref, p_ref, wd_ref, h_ref, w_s):
+    @pl.when(pl.program_id(0) == 0)
+    def _():
+        for c in range(NCH):
+            w_s[pl.ds(c * CW, CW), :] = wd_ref[:, c].reshape(CW, D)
+
+    for i in range(TB // SUB):
+        rows = pl.ds(i * SUB, SUB)
+        h_ref[rows, :] = x_ref[rows, :] + dot(p_ref[rows, :], w_s[...], 1, 0).astype(BF16)
+
+
+def down(x, p, wd):
+    return pl.pallas_call(
+        down_kernel,
+        grid=(TOK // TB,),
+        in_specs=[
+            pl.BlockSpec((TB, D), lambda t: (t, 0)),
+            pl.BlockSpec((TB, FF), lambda t: (t, 0)),
+            pl.BlockSpec((DP, NCH, KR, D), lambda t: (0, 0, 0, 0)),
+        ],
+        out_specs=pl.BlockSpec((TB, D), lambda t: (t, 0)),
+        out_shape=jax.ShapeDtypeStruct((TOK, D), BF16),
+        scratch_shapes=[pltpu.VMEM((FF, D), BF16)],
+        compiler_params=pltpu.CompilerParams(vmem_limit_bytes=VMEM_LIMIT, dimension_semantics=("arbitrary",)),
+        cost_estimate=pl.CostEstimate(flops=2 * TOK * D * FF, bytes_accessed=4 * 10**7, transcendentals=0),
+        name="down",
+    )(x, p, wd)
 
 
 def backward_kernel(
-    x_ref, h_ref, dy_ref, g_ref, u_ref, wg_ref, wu_ref, wd_ref,
+    x_ref, h_ref, a_ref, dy_ref, g_ref, u_ref, wg2_ref, wu2_ref, wd2_ref, wg1_ref, wu1_ref, wd1_ref,
     dx_ref, ogu_ref, od_ref,
-    a_s, dcur, da, p_s, dg_s, du_s, acc_g, acc_u, acc_d,
+    wg_s, wu_s, wd_s, dcur, da, p_s, dg_s, du_s, acc_g, acc_u, acc_d,
     st_gu, st_d, xs_gu, xs_d, xr_gu, xr_d, cs_gu, cs_d, cr_gu, cr_d, fo_gu, fo_d,
     in_sem, xs_sem, xr_sem, cs_sem, cr_sem, out_sem, xfree, cfree,
 ):
@@ -265,40 +284,24 @@
         c = p % NCH
         tok = pl.multiple_of(t * T, T)
 
-        def norm_into(src):
-            for i in range(T // SUB):
-                rows = pl.ds(i * SUB, SUB)
-                h = src[rows, :].astype(F32)
-                a_s[rows, :] = (h * scale_of(h)).astype(BF16)
-
-        wg = wg_ref[...].reshape(D, CW)
-        wu = wu_ref[...].reshape(D, CW)
-        wd = wd_ref[...].reshape(CW, D)
-
-        def elementwise(g, u, i):
+        for mine, of_layer in ((p < NCH, (wg2_ref, wu2_ref, wd2_ref)), (p >= NCH, (wg1_ref, wu1_ref, wd1_ref))):
+            @pl.when(mine & (t == 0))
+            def _(of_layer=of_layer):
+                wg_s[...] = of_layer[0][...].reshape(D, CW)
+                wu_s[...] = of_layer[1][...].reshape(D, CW)
+                wd_s[...] = of_layer[2][...].reshape(CW, D)
+
+        for i in range(T // SUB):
             rows = pl.ds(i * SUB, SUB)
-            dp = dot(dcur[pl.ds(tok + i * SUB, SUB), :], wd, 1, 1).astype(BF16).astype(F32)
+            g, u = g_ref[rows, :], u_ref[rows, :]
+            dp = dot(dcur[pl.ds(tok + i * SUB, SUB), :], wd_s[...], 1, 1).astype(BF16).astype(F32)
             s = sigmoid(g)
             act = g * s
             p_s[rows, :] = (act * u).astype(BF16)
             du_s[rows, :] = (act * dp).astype(BF16)
             dg_s[rows, :] = (dp * u * (s + act * (1.0 - s))).astype(BF16)
 
-        @pl.when(p < NCH)
-        def _():
-            norm_into(h_ref)
-            for i in range(T // SUB):
-                a = a_s[pl.ds(i * SUB, SUB), :]
-                elementwise(dot(a, wg, 1, 0), dot(a, wu, 1, 0), i)
-
-        @pl.when(p >= NCH)
-        def _():
-            norm_into(x_ref)
-            for i in range(T // SUB):
-                rows = pl.ds(i * SUB, SUB)
-                elementwise(g_ref[rows, :], u_ref[rows, :], i)
-
-        a = a_s[...]
+        a, wg, wu = a_ref[...], wg_s[...], wu_s[...]
         here = pl.ds(tok, T)
         acc_d[...] += dot(p_s[...], dcur[here, :], 0, 0)
         acc_g[...] += dot(a, dg_s[...], 0, 0)
@@ -372,30 +375,43 @@
                 cp.wait()
 
 
-def backward(x, h, dy, g, u, wg, wu, wd):
+def backward(x, h, a, dy, g, u, wgu1, wd1, wgu2, wd2):
     def phase(p):
         return jnp.minimum(p, NP - 1)
 
-    def w_map(p, t):
-        q = phase(p)
-        return (0, 1 - q // NCH, q % NCH, 0, 0)
-
-    late = lambda p, t: jnp.where(p >= NP, NT - 1, jnp.where(p >= NCH, t, 0))
-    gu_spec = pl.BlockSpec((T, CW), lambda p, t: (late(p, t), jnp.where(p >= NCH, phase(p) % NCH, 0)))
+    def chunk(lay, p):
+        return jnp.minimum(p, NCH - 1) if lay else jnp.maximum(phase(p) - NCH, 0)
+
+    def w_specs(lay):
+        return [
+            pl.BlockSpec((DP, None, DR, CW), lambda p, t: (0, chunk(lay, p), 0, 0)),
+            pl.BlockSpec((DP, None, DR, CW), lambda p, t: (0, NCH + chunk(lay, p), 0, 0)),
+            pl.BlockSpec((DP, None, KR, D), lambda p, t: (0, chunk(lay, p), 0, 0)),
+        ]
+
+    layer = lambda p: 1 - phase(p) // NCH
+    row = lambda p, t: jnp.where(p >= NP, NT - 1, t)
+    gu_spec = pl.BlockSpec((None, T, CW), lambda p, t: (layer(p), row(p, t), phase(p) % NCH))
     any_spec = pl.BlockSpec(memory_space=pl.ANY)
     vm = pltpu.VMEM
     return pl.pallas_call(
         backward_kernel,
         grid=(NP + 2, NT),
         in_specs=[
-            pl.BlockSpec((T, D), lambda p, t: (late(p, t), 0)),
-            pl.BlockSpec((T, D), lambda p, t: (jnp.where(p < NCH, t, NT - 1), 0)),
+            pl.BlockSpec(
+                (T, D), lambda p, t: (jnp.where(p >= NP, NT - 1, jnp.where(p == NP - 1, t, 0)), 0),
+                pipeline_mode=pl.Buffered(1),
+            ),
+            pl.BlockSpec(
+                (T, D), lambda p, t: (jnp.where(p >= NCH, NT - 1, jnp.where(p == NCH - 1, t, 0)), 0),
+                pipeline_mode=pl.Buffered(1),
+            ),
+            pl.BlockSpec((None, T, D), lambda p, t: (layer(p), row(p, t), 0)),
             any_spec,
             gu_spec,
             gu_spec,
-            pl.BlockSpec((DP, None, None, DR, CW), w_map),
-            pl.BlockSpec((DP, None, None, DR, CW), w_map),
-            pl.BlockSpec((DP, None, None, KR, D), w_map),
+            *w_specs(1),
+            *w_specs(0),
         ],
         out_specs=[
             pl.BlockSpec((T, D), lambda p, t: (jnp.where(p >= NP, NT - 1, jnp.where(p == NP - 1, t, 0)), 0)),
@@ -408,7 +424,7 @@
             jax.ShapeDtypeStruct((L, NCH, KR, D), BF16),
         ],
         scratch_shapes=[
-            vm((T, D), BF16), vm((TOK, D), BF16), vm((TOK, D), F32),
+            vm((D, CW), BF16), vm((D, CW), BF16), vm((CW, D), BF16), vm((TOK, D), BF16), vm((TOK, D), F32),
             vm((T, CW), BF16), vm((T, CW), BF16), vm((T, CW), BF16),
             vm((D, CW), F32), vm((D, CW), F32), vm((CW, D), F32),
             vm((2, 4, 2, DR, CW), F32), vm((2, 4, KR, D), F32),
@@ -429,18 +445,23 @@
         ),
         cost_estimate=pl.CostEstimate(flops=28 * TOK * D * FF, bytes_accessed=10**8, transcendentals=0),
         name="backward",
-    )(x, h, dy, g, u, wg, wu, wd)
+    )(x, h, a, dy, g, u, wgu2, wgu2, wd2, wgu1, wgu1, wd1)
 
 
 def solution(mesh):
     def body(x, dy, w_gate, w_up, w_down):
         x, dy = x[0], dy[0]
-        split = lambda w: w.reshape(L, DR, DP, NCH, KR).transpose(0, 3, 1, 2, 4).reshape(L, NCH, DR, CW)
+        split = lambda w: w.reshape(DR, DP, NCH, KR).transpose(2, 0, 1, 3).reshape(NCH, DR, CW)
         gather = lambda w: lax.all_gather(w, "dp", axis=0, tiled=False)
-        wg, wu = gather(split(w_gate)), gather(split(w_up))
-        wd = gather(w_down.reshape(L, NCH, KR, D))
-        g, u, h = forward(x, wg, wu, wd)
-        dx, ogu, od = backward(x, h, dy, g, u, wg, wu, wd)
+        w_down = w_down.reshape(L, NCH, KR, D)
+        wgu1 = gather(jnp.concatenate([split(w_gate[0]), split(w_up[0])]))
+        wd1 = gather(w_down[0])
+        wgu2 = gather(jnp.concatenate([split(w_gate[1]), split(w_up[1])]))
+        wd2 = gather(w_down[1])
+        g, u, a, p = gate_up(0, x, wgu1)
+        h = down(x, p, wd1)
+        g, u, a = gate_up(1, h, wgu2, g, u, a)
+        dx, ogu, od = backward(x, h, a, dy, g, u, wgu1, wd1, wgu2, wd2)
         join = lambda o: o.reshape(L, NCH, DR, DP, KR).transpose(0, 2, 3, 1, 4).reshape(L, DR, FF)
         return dx[None], join(ogu[:, :, 0]), join(ogu[:, :, 1]), od.reshape(L, NCH * KR, D)
 

time: 786 us -> 668 us (0.85)
  waiting for transfers between devices: 243 us -> 115 us
    all_gather x3 -> x4, waiting for transfers between devices: 242 us -> 115 us  [body(): gather = lambda w: lax.all_gather(w, 'dp', axis=0, tiled=False)]
    pallas_call x1 -> x3, Pallas kernels: 93.5 us -> 156 us  [the longest x2 131 us: gate_up(): pl.pallas_call(functools.partial(gate_up_kernel, keep_p), grid=(NT, NCH),...]
    pallas_call x1, Pallas kernels: 415 us -> 356 us  [backward(): pl.pallas_call(backward_kernel, grid=(NP + 2, NT), in_specs=[pl.BlockSpec...]
  transfers between devices with their start and end apart: 3 -> 4, of which waited for: 3 -> 2; matrix products, arithmetic and copies ran while one was open for 1% -> 1% of each run, Pallas kernels for 0% -> 23%
where the time goes in v2:
time: 668 us; the launch traced here: 665 us
  Pallas kernels  512 us (77%)
  waiting for transfers between devices  115 us (17%)
  local copies, waits for them, and re-layouts  23.1 us (3%)
  between operations  13.9 us (2%)
    pallas_call x1, Pallas kernels, backward(): pl.pallas_call(backward_kernel, grid=(NP + 2, NT), in_specs=[pl.BlockSpec...  356 us
    pallas_call x2, Pallas kernels, gate_up(): pl.pallas_call(functools.partial(gate_up_kernel, keep_p), grid=(NT, NCH),...  131 us
    all_gather x4, waiting for transfers between devices, body(): gather = lambda w: lax.all_gather(w, 'dp', axis=0, tiled=False)  115 us
    pallas_call x1, Pallas kernels, down(): pl.pallas_call(down_kernel, grid=(TOK // TB,), in_specs=[pl.BlockSpec((TB...  25.6 us
  transfers between devices with their start and end apart: 4, of which 2 were waited for; matrix products, arithmetic and copies ran while one was open for 1% of the time, Pallas kernels for 23%

profile of v2, /device:TPU:0, one launch (start us, length us, event | category | flops | bytes accessed | tf_op | source)
XLA Modules:
  0.0 665.3 jit_solution(5705985132016251578)
XLA Ops:
  7.2 1.3 fusion.2
  8.5 0.3 copy.50
  8.8 0.1 copy.35
  8.9 1.3 fusion.3
  10.1 0.3 copy.51
  10.5 0.1 copy.37
  10.5 0.2 pad_maximum_fusion
  10.8 1.4 copy.38
  12.2 2.2 fusion.1
  14.5 0.0 all-gather.13.cloned.1.call-start
  14.5 0.3 copy.52
  14.8 0.1 copy.40
  14.9 0.3 copy.53
  15.2 0.1 copy.42
  15.3 0.2 pad_maximum_fusion.1
  15.5 1.4 copy.43
  17.0 0.5 all-gather.9.cloned.1.call-update
  17.5 77.9 %all-gather.11.cloned.1.call-done = bf16[144,112,256]{2,1,0:T(8,128)(2,1)} async-done(((bf16[18,112,256]{2,1,0:T(8,128)(2,1)}), bf16[144,112,256]{2,1,0:T(8,128)(2,1)}) %all-gather.11.cloned.1.call-update) | async-done | bytes 8257552 | tf_op jit(solution)/shard_map/all_gather | solution.py:455
  95.4 66.4 %gate_up_0.1 = (f32[2,4096,2304]{2,1,0:T(8,128)}, f32[2,4096,2304]{2,1,0:T(8,128)}, bf16[2,4096,896]{2,1,0:T(8,128)(2,1)}, bf16[4096,2304]{1,0:T(8,128)(2,1)}) custom-call(bf16[4096,896]{1,0:T(8,128)(2,1)} %bitcast.56, bf16[8,18,112,256]{3,2,1,0:T(8,128)(2,1)} %bitcast.52, bf16[8,18,112,256]{3,2,1,0:T(8,128)(2,1)} %bitcast.53), custom_call_target="tpu_custom_call" | custom-call | flops 33822867456 | bytes 100000000 | tf_op jit(solution)/shard_map/gate_up_0/pallas_call | solution.py:67
  161.9 25.6 %down.1.x_ref.h_ref = bf16[4096,896]{1,0:T(8,128)(2,1)} custom-call(bf16[4096,896]{1,0:T(8,128)(2,1)} %bitcast.57, bf16[4096,2304]{1,0:T(8,128)(2,1)} %get-tuple-element.14.p_ref, bf16[8,9,32,896]{3,2,1,0:T(8,128)(2,1)} %all-gather.7.cloned.1.call-done.wd_ref.wd1_ref), custom_call_target="tpu_custom_call" | custom-call | flops 16911433728 | bytes 40000000 | tf_op jit(solution)/shard_map/down/pallas_call | solution.py:98
  187.4 36.8 %all-gather.13.cloned.1.call-done = bf16[144,112,256]{2,1,0:T(8,128)(2,1)} async-done(((bf16[18,112,256]{2,1,0:T(8,128)(2,1)}), bf16[144,112,256]{2,1,0:T(8,128)(2,1)}) %all-gather.13.cloned.1.call-update) | async-done | bytes 8257552 | tf_op jit(solution)/shard_map/all_gather | solution.py:455
  224.3 64.2 %gate_up_1.1 = (f32[2,4096,2304]{2,1,0:T(8,128)}, f32[2,4096,2304]{2,1,0:T(8,128)}, bf16[2,4096,896]{2,1,0:T(8,128)(2,1)}) custom-call(bf16[4096,896]{1,0:T(8,128)(2,1)} %down.1.x_ref.h_ref, bf16[8,18,112,256]{3,2,1,0:T(8,128)(2,1)} %bitcast.32, bf16[8,18,112,256]{3,2,1,0:T(8,128)(2,1)} %bitcast.33, ...), custom_call_target="tpu_custom_call", output_to_operand_aliasing={{0}: (3, {}), {1}: (4, {}), {2}: (5, {})} | custom-call | flops 33822867456 | bytes 100000000 | tf_op jit(solution)/shard_map/gate_up_1/pallas_call | solution.py:67
  288.4 356.2 %backward.1 = (bf16[4096,896]{1,0:T(8,128)(2,1)}, bf16[2,9,2,112,256]{4,3,2,1,0:T(8,128)(2,1)}, bf16[2,9,32,896]{3,2,1,0:T(8,128)(2,1)}) custom-call(bf16[4096,896]{1,0:T(8,128)(2,1)} %bitcast.58, bf16[4096,896]{1,0:T(8,128)(2,1)} %down.1.x_ref.h_ref, bf16[2,4096,896]{2,1,0:T(8,128)(2,1)} %get-tuple-element.18.a_ref, bf16[4096,896]{1,0:T(8,128)(2,1)} %bitcast.59, ...), custom_call_target="tpu_custom_call" | custom-call | flops 236760072192 | bytes 100000000 | tf_op jit(solution)/shard_map/backward/pallas_call | solution.py:397
  644.6 1.7 fusion
  646.3 0.8 copy.44
  647.1 0.2 copy.45
  647.3 1.4 copy.48
  648.7 0.7 copy.46
  649.4 0.2 copy.47
  649.6 1.4 copy.49
  651.0 6.8 %copy.59 = bf16[1,4096,896]{2,1,0:T(8,128)(2,1)} copy(bf16[1,4096,896]{2,1,0:T(8,128)(2,1)} %bitcast.36) | data formatting | bytes 14680064
  657.8 1.0 copy.60
  (10 shorter events, 0.2 us)
Async XLA Ops:
  7.2 88.3 %all-gather.11.cloned.1.call-start = ((), (), s32[]{:S(2)}) async-start(), calls=%async_computation.2 | async-start | bytes 9289728 | tf_op jit(solution)/shard_map/all_gather | solution.py:455
  12.2 149.7 %all-gather.7.cloned.1.call-start = ((), (), s32[]{:S(2)}) async-start(), calls=%async_computation | async-start | bytes 4644864 | tf_op jit(solution)/shard_map/all_gather | solution.py:455
  14.5 209.8 %all-gather.13.cloned.1.call-start = ((), (), s32[]{:S(2)}) async-start(), calls=%async_computation.3 | async-start | bytes 9289728 | tf_op jit(solution)/shard_map/all_gather | solution.py:455
  16.9 271.5 %all-gather.9.cloned.1.call-start = ((), (), s32[]{:S(2)}) async-start(), calls=%async_computation.1 | async-start | bytes 4644864 | tf_op jit(solution)/shard_map/all_gather | solution.py:455
  651.0 6.8 %copy-start = (bf16[2,9,32,896]{3,2,1,0:T(8,128)(2,1)S(1)}, bf16[2,9,32,896]{3,2,1,0:T(8,128)(2,1)}, u32[]{:S(2)}) copy-start(bf16[2,9,32,896]{3,2,1,0:T(8,128)(2,1)} %get-tuple-element.23) | copy-start | bytes 3096580
Sparse Core Ops, SparseCore 0:
  12.3 83.1 all-gather.10
  97.6 44.8 all-gather.6
  144.8 79.4 all-gather.12
  226.3 44.8 all-gather.8
